TPU v7x, 32 devices: a whole 2x2x4 slice. The times are simulated.
32 devices in a mesh: head: 2 (over x), inner: 4 (over y, core), outer: 4 (over z).
Axes of the slice: x: 2, y: 2, z: 4, core: 2. Of those that a mesh axis runs over, the one named last changes fastest.
Arguments:
- queries: float32 [2048, 8, 128], P(('inner', 'outer'), 'head'), may hold values from -8 to 8
- key_rows: float32 [2048, 128], P(('inner', 'outer'), 'head'), may hold values from -8 to 8
- values: float32 [2048, 128], P(('inner', 'outer'), 'head'), may hold values from -24 to 24
- out_grad: float32 [2048, 8, 128], P(('inner', 'outer'), 'head'), may hold values from -48 to 48
- sink_len: int32 [1], replicated, may hold values from 32 to 128
- window_len: int32 [1], replicated, may hold values from 129 to 640
- block_codes: int32 [16, 5], replicated, may hold values from 0 to 2, as said below
Outputs:
- query_grad: float32 [2048, 8, 128], P(('inner', 'outer'), 'head')
- key_grad: float32 [2048, 128], P(('inner', 'outer'), 'head')
- value_grad: float32 [2048, 128], P(('inner', 'outer'), 'head')
Inputs may be any that keep to these rules, and one draw needn't show every extreme that they name: block_codes[b, 0] is 1 or 2 for every block b.
All inputs are finite; a program needn't handle non-finite values.
Results may differ from a plain program's by a relative error of at most 0.0003.
Values sent between devices are 32-bit elements; how exact they have to be, the bound alone decides.
A program may use at most 64 MiB of HBM per device.

v0:
```python
import math
import jax
import jax.numpy as jnp
from jax import lax
from jax.sharding import PartitionSpec as P

STEPS = 5
SINK = 128
very_low = -1e30
precise = lax.Precision.HIGHEST


def swapped(array, axis, distance):
    return lax.ppermute(array, axis, [(i, i ^ 1 << distance) for i in range(lax.axis_size(axis))])


def spread(array, axis, root):
    mine = lax.axis_index(axis) == root
    return lax.psum(jnp.where(mine, array, jnp.zeros_like(array)), axis)


def shifted(value, axis, steps):
    count = lax.axis_size(axis)
    pairs = [(source, (source + steps) % count) for source in range(count)]
    return lax.ppermute(value, axis, pairs)


def codes_for(block_codes, query_block, offset):
    row_ids = jnp.arange(block_codes.shape[0], dtype=jnp.int32)
    return jnp.sum(jnp.where(row_ids == query_block, block_codes[:, offset], 0))


def visible(query_block, key_block, offset, block_rows, sink_end, window, block_codes, present):
    local_ids = jnp.arange(block_rows, dtype=jnp.int32)
    pos_q = query_block * block_rows + local_ids
    pos_k = key_block * block_rows + local_ids
    code = codes_for(block_codes, query_block, offset)
    near = pos_q[:, None] - pos_k[None, :] < window
    rule = (code != 0) & ((code == 2) | near)
    in_sink = (pos_k < sink_end)[None, :]
    chosen = jnp.where(query_block == 0, in_sink | rule, jnp.logical_not(in_sink) & rule)
    return present & (pos_k[None, :] <= pos_q[:, None]) & chosen


def scores(query_blk, key_blk, temper):
    return temper * jnp.einsum("qhd,kd->hqk", query_blk, key_blk, precision=precise)


def forward_step(running, query_blk, key_blk, value_blk, allowed, temper):
    row_max, row_sum, carried = running
    logits = jnp.where(allowed[None], scores(query_blk, key_blk, temper), very_low)
    new_max = jnp.maximum(row_max, jnp.max(logits, axis=2))
    factor = jnp.exp(row_max - new_max)
    weights = jnp.where(allowed[None], jnp.exp(logits - new_max[:, :, None]), 0.0)
    row_sum = row_sum * factor + jnp.sum(weights, axis=2)
    carried = carried * factor[:, :, None] + jnp.einsum(
        "hqk,kd->hqd", weights, value_blk, precision=precise
    )
    return ((new_max, row_sum, carried), logits)


def finish(running, grad_blk):
    row_max, row_sum, carried = running
    log_sum = row_max + jnp.log(row_sum)
    row_delta = jnp.sum(jnp.transpose(grad_blk, (1, 0, 2)) * carried, axis=2) / row_sum
    return (log_sum, row_delta)


def backward_step(
    query_blk, grad_blk, log_sum, row_delta, key_blk, value_blk, allowed, temper, cached
):
    if cached is None:
        cached = scores(query_blk, key_blk, temper)
    weights = jnp.where(allowed[None], jnp.exp(cached - log_sum[:, :, None]), 0.0)
    grad_dots = jnp.einsum("qhd,kd->hqk", grad_blk, value_blk, precision=precise)
    dscores = weights * (grad_dots - row_delta[:, :, None])
    step_dq = temper * jnp.einsum("hqk,kd->qhd", dscores, key_blk, precision=precise)
    step_dk = temper * jnp.einsum("hqk,qhd->kd", dscores, query_blk, precision=precise)
    step_dv = jnp.einsum("hqk,qhd->kd", weights, grad_blk, precision=precise)
    return (step_dq, step_dk, step_dv)


def shards(queries, key_rows, values, out_grad, sink_len, window_len, block_codes):
    block_rows, heads_dev, head_dim = queries.shape
    temper = 1.0 / math.sqrt(head_dim)
    sink_end = sink_len[0]
    window = window_len[0]
    seq_index = lax.axis_index(("inner", "outer"))
    seq_count = lax.axis_size(("inner", "outer"))
    upper_half = lax.axis_index("head") % 2 == 1
    other_keys, other_values = swapped((key_rows, values), "head", 0)
    key_full = jnp.where(
        upper_half,
        jnp.concatenate([other_keys, key_rows], 1),
        jnp.concatenate([key_rows, other_keys], 1),
    )
    value_full = jnp.where(
        upper_half,
        jnp.concatenate([other_values, values], 1),
        jnp.concatenate([values, other_values], 1),
    )
    sink_keys, sink_values = (
        spread(key_full, ("inner", "outer"), 0),
        spread(value_full, ("inner", "outer"), 0),
    )
    sink_ids = jnp.arange(SINK, dtype=jnp.int32)
    sink_allowed = jnp.broadcast_to(
        ((seq_index >= 1) & (sink_ids < sink_end))[None, :], (block_rows, SINK)
    )
    carried = jnp.zeros((heads_dev, block_rows, head_dim), jnp.float32)
    running = (
        jnp.full((heads_dev, block_rows), very_low, jnp.float32),
        jnp.zeros((heads_dev, block_rows), jnp.float32),
        carried,
    )
    running, ignored = forward_step(running, queries, sink_keys, sink_values, sink_allowed, temper)
    grad_keys = jnp.zeros((block_rows, head_dim), jnp.float32)
    grad_values = jnp.zeros((block_rows, head_dim), jnp.float32)
    moving_k, moving_v = (key_full, value_full)
    cached = None
    for offset in range(STEPS):
        if offset > 0:
            moving_k, moving_v = shifted((moving_k, moving_v), ("inner", "outer"), 1)
        allowed = visible(
            seq_index,
            (seq_index - offset) % seq_count,
            offset,
            block_rows,
            sink_end,
            window,
            block_codes,
            seq_index - offset >= 0,
        )
        running, cached = forward_step(running, queries, moving_k, moving_v, allowed, temper)
    log_sum, row_delta = finish(running, out_grad)
    grad_q = jnp.zeros_like(queries)
    for offset in range(STEPS - 1, -1, -1):
        if offset < STEPS - 1:
            moving_k, moving_v, grad_keys, grad_values = shifted(
                (moving_k, moving_v, grad_keys, grad_values), ("inner", "outer"), -1
            )
            cached = None
        allowed = visible(
            seq_index,
            (seq_index - offset) % seq_count,
            offset,
            block_rows,
            sink_end,
            window,
            block_codes,
            seq_index - offset >= 0,
        )
        step_dq, step_dk, step_dv = backward_step(
            queries, out_grad, log_sum, row_delta, moving_k, moving_v, allowed, temper, cached
        )
        grad_q = grad_q + step_dq
        grad_keys = grad_keys + step_dk
        grad_values = grad_values + step_dv
    sink_dq, sink_dk, sink_dv = backward_step(
        queries, out_grad, log_sum, row_delta, sink_keys, sink_values, sink_allowed, temper, None
    )
    grad_q = grad_q + sink_dq
    total_dk, total_dv = lax.psum((sink_dk, sink_dv), ("inner", "outer"))
    is_first = seq_index == 0
    grad_keys = grad_keys.at[:SINK].add(jnp.where(is_first, total_dk, 0.0))
    grad_values = grad_values.at[:SINK].add(jnp.where(is_first, total_dv, 0.0))
    half_cols = key_rows.shape[1]
    keep_k = jnp.where(upper_half, grad_keys[:, half_cols:], grad_keys[:, :half_cols])
    send_k = jnp.where(upper_half, grad_keys[:, :half_cols], grad_keys[:, half_cols:])
    keep_v = jnp.where(upper_half, grad_values[:, half_cols:], grad_values[:, :half_cols])
    send_v = jnp.where(upper_half, grad_values[:, :half_cols], grad_values[:, half_cols:])
    got_k, got_v = swapped((send_k, send_v), "head", 0)
    return (grad_q, keep_k + got_k, keep_v + got_v)


def solution(mesh):
    in_specs = (
        P(("inner", "outer"), "head", None),
        P(("inner", "outer"), "head"),
        P(("inner", "outer"), "head"),
        P(("inner", "outer"), "head", None),
        P(),
        P(),
        P(),
    )
    out_specs = (
        P(("inner", "outer"), "head", None),
        P(("inner", "outer"), "head"),
        P(("inner", "outer"), "head"),
    )
    return jax.shard_map(shards, mesh=mesh, in_specs=in_specs, out_specs=out_specs, check_vma=False)
```

profile of v0, /device:TPU:8, one launch (start us, length us, event | category | flops | bytes accessed | tf_op | source)
XLA Modules:
  0.0 250.2 jit_solution(6072486249846511252)
XLA Ops:
  7.2 0.9 copy.10
  8.1 1.6 collective-permute-start
  9.8 0.6 collective-permute-start.5
  10.4 0.7 copy-done.6
  11.1 0.7 fusion.159
  20.8 0.7 broadcast_select_fusion.1
  21.6 1.6 collective-permute-start.1
  23.2 0.7 broadcast_select_fusion
  23.9 1.6 collective-permute-start.6
  26.2 1.6 collective-permute-start.2
  28.2 88.4 %all-reduce.7.cloned.1.call-done = (f32[128,128]{1,0:T(8,128)}, f32[128,128]{1,0:T(8,128)}) async-done(((f32[128,128]{1,0:T(8,128)}, f32[128,128]{1,0:T(8,128)}), (f32[128,128]{1,0:T(8,128)}, f32[128,128]{1,0:T(8,128)})) %all-reduce.7.cloned.1.call-update) | async-done | bytes 131088 | tf_op jit(solution)/shard_map/psum | solution.py:19
  116.6 1.2 select_reduce_fusion
  117.9 2.0 collective-permute-start.3
  120.3 1.8 collective-permute-done.7
  122.2 0.7 collective-permute-done.3
  122.9 1.3 collective-permute-start.4
  124.6 1.8 collective-permute-done.8
  126.4 0.7 collective-permute-start.9
  127.2 1.4 collective-permute-done.4
  129.5 0.4 convolution_bitcast_fusion.11
  130.4 0.5 fusion.20
  131.3 0.4 fusion.18
  131.8 0.4 fusion.17
  132.2 0.4 fusion.16
  132.7 1.1 convolution_bitcast_fusion.6
  133.7 0.4 fusion.48
  134.6 1.0 fusion.49
  136.0 4.2 %collective-permute-start.23 = (f32[128,128]{1,0:T(8,128)S(1)}, f32[128,128]{1,0:T(8,128)S(1)}, u32[]{:S(2)}, u32[]{:S(2)}) collective-permute-start(f32[128,128]{1,0:T(8,128)S(1)} %convolution_bitcast_fusion.11), channel_id=1, source_target_pairs={{0,15},{1,0},{2,1},{3,2},{4,3},{5,4},{6,5},{7,6},{8,7},{9,8},{10,9... | collective-permute-start | bytes 196616 | tf_op jit(solution)/shard_map/ppermute | solution.py:25
  141.0 1.1 collective-permute-start.18
  142.7 3.8 %collective-permute-done.10 = f32[128,128]{1,0:T(8,128)S(1)} collective-permute-done((f32[128,128]{1,0:T(8,128)S(1)}, f32[128,128]{1,0:T(8,128)S(1)}, u32[]{:S(2)}, u32[]{:S(2)}) %collective-permute-start.10) | collective-permute-done | bytes 65568 | tf_op jit(solution)/shard_map/ppermute | solution.py:25
  147.3 1.3 collective-permute-start.24
  149.4 2.3 collective-permute-start.19
  152.3 4.2 %collective-permute-done.12 = f32[128,128]{1,0:T(8,128)S(1)} collective-permute-done((f32[128,128]{1,0:T(8,128)S(1)}, f32[128,128]{1,0:T(8,128)S(1)}, u32[]{:S(2)}, u32[]{:S(2)}) %collective-permute-start.12) | collective-permute-done | bytes 65568 | tf_op jit(solution)/shard_map/ppermute | solution.py:25
  157.3 1.8 collective-permute-start.25
  159.9 1.9 collective-permute-start.20
  161.9 0.5 collective-permute-start.14
  162.9 3.8 %collective-permute-done.14 = f32[128,128]{1,0:T(8,128)S(1)} collective-permute-done((f32[128,128]{1,0:T(8,128)S(1)}, f32[128,128]{1,0:T(8,128)S(1)}, u32[]{:S(2)}, u32[]{:S(2)}) %collective-permute-start.14) | collective-permute-done | bytes 65568 | tf_op jit(solution)/shard_map/ppermute | solution.py:25
  167.6 1.7 collective-permute-start.26
  170.1 2.8 %collective-permute-start.21 = (f32[128,128]{1,0:T(8,128)S(1)}, f32[128,128]{1,0:T(8,128)S(1)}, u32[]{:S(2)}, u32[]{:S(2)}) collective-permute-start(f32[128,128]{1,0:T(8,128)S(1)} %add.352), channel_id=1, source_target_pairs={{0,15},{1,0},{2,1},{3,2},{4,3},{5,4},{6,5},{7,6},{8,7},{9,8},{10,9... | collective-permute-start | bytes 196616 | tf_op jit(solution)/shard_map/ppermute | solution.py:25
  173.6 3.6 %collective-permute-done.16 = f32[128,128]{1,0:T(8,128)S(1)} collective-permute-done((f32[128,128]{1,0:T(8,128)S(1)}, f32[128,128]{1,0:T(8,128)S(1)}, u32[]{:S(2)}, u32[]{:S(2)}) %collective-permute-start.16) | collective-permute-done | bytes 65568 | tf_op jit(solution)/shard_map/ppermute | solution.py:25
  177.9 57.4 %all-reduce.5.cloned.1.call-done = (f32[128,128]{1,0:T(8,128)}, f32[128,128]{1,0:T(8,128)}) async-done(((f32[128,128]{1,0:T(8,128)}, f32[128,128]{1,0:T(8,128)}), (f32[128,128]{1,0:T(8,128)}, f32[128,128]{1,0:T(8,128)})) %all-reduce.5.cloned.1.call-update) | async-done | bytes 131088 | tf_op jit(solution)/shard_map/psum | solution.py:163
  235.4 1.5 collective-permute-start.27
  238.3 0.6 collective-permute-start.22
  238.9 0.4 fusion.2
  239.4 0.8 copy.78
  240.3 0.7 copy.80
  241.0 1.6 collective-permute-done.22
  242.7 0.7 copy.79
  (112 shorter events, 16.2 us)
Async XLA Ops:
  7.2 18.3 %copy-start = (f32[128,4,128]{2,1,0:T(4,128)S(1)}, f32[128,4,128]{2,1,0:T(4,128)}, u32[]{:S(2)}) copy-start(f32[128,4,128]{2,1,0:T(4,128)} %param.15) | copy-start | bytes 786436
  7.2 2.5 copy-start.5
  7.2 109.4 %all-reduce.7.cloned.1.call-start = ((), (), s32[]{:S(2)}) async-start(), calls=%async_computation.1 | async-start | bytes 262144 | tf_op jit(solution)/shard_map/psum | solution.py:19
  8.1 12.7 %collective-permute-start = (f32[128,64]{1,0:T(8,128)S(1)}, f32[128,64]{1,0:T(8,128)S(1)}, u32[]{:S(2)}, u32[]{:S(2)}) collective-permute-start(f32[128,64]{1,0:T(8,128)S(1)} %copy.10), channel_id=1, source_target_pairs={{0,16},{16,0},{1,17},{17,1},{2,18},{18,2},{3,19},{19,3},{4,20},{20... | collective-permute-start | bytes 98312 | tf_op jit(solution)/shard_map/ppermute | solution.py:14
  9.8 13.4 %collective-permute-start.5 = (f32[128,64]{1,0:T(8,128)S(1)}, f32[128,64]{1,0:T(8,128)S(1)}, u32[]{:S(2)}, u32[]{:S(2)}) collective-permute-start(f32[128,64]{1,0:T(8,128)S(1)} %copy.24), channel_id=1, source_target_pairs={{0,16},{16,0},{1,17},{17,1},{2,18},{18,2},{3,19},{19,3},{4,20},{20... | collective-permute-start | bytes 98312 | tf_op jit(solution)/shard_map/ppermute | solution.py:14
  10.4 0.7 copy-start.6
  10.4 10.3 %copy-start.1 = (f32[128,4,128]{2,1,0:T(4,128)S(1)}, f32[128,4,128]{2,1,0:T(4,128)}, u32[]{:S(2)}) copy-start(f32[128,4,128]{2,1,0:T(4,128)} %param.18) | copy-start | bytes 786436
  21.6 4.6 %collective-permute-start.1 = (f32[128,128]{1,0:T(8,128)S(1)}, f32[128,128]{1,0:T(8,128)S(1)}, u32[]{:S(2)}, u32[]{:S(2)}) collective-permute-start(f32[128,128]{1,0:T(8,128)S(1)} %get-tuple-element.80), channel_id=1, source_target_pairs={{0,1},{1,2},{2,3},{3,4},{4,5},{5,6},{6,7},{7,8},{8,9},{9,10},{10,1... | collective-permute-start | bytes 196616 | tf_op jit(solution)/shard_map/ppermute | solution.py:25
  23.9 94.0 %collective-permute-start.6 = (f32[128,128]{1,0:T(8,128)S(1)}, f32[128,128]{1,0:T(8,128)S(1)}, u32[]{:S(2)}, u32[]{:S(2)}) collective-permute-start(f32[128,128]{1,0:T(8,128)S(1)} %get-tuple-element.78), channel_id=1, source_target_pairs={{0,1},{1,2},{2,3},{3,4},{4,5},{5,6},{6,7},{7,8},{8,9},{9,10},{10,1... | collective-permute-start | bytes 196616 | tf_op jit(solution)/shard_map/ppermute | solution.py:25
  25.9 209.4 %all-reduce.5.cloned.1.call-start = ((), (), s32[]{:S(2)}) async-start(), calls=%async_computation | async-start | bytes 262144 | tf_op jit(solution)/shard_map/psum | solution.py:163
  26.2 91.7 %collective-permute-start.2 = (f32[128,128]{1,0:T(8,128)S(1)}, f32[128,128]{1,0:T(8,128)S(1)}, u32[]{:S(2)}, u32[]{:S(2)}) collective-permute-start(f32[128,128]{1,0:T(8,128)S(1)} %collective-permute-done.1), channel_id=1, source_target_pairs={{0,1},{1,2},{2,3},{3,4},{4,5},{5,6},{6,7},{7,8},{8,9},{9,10},{10,1... | collective-permute-start | bytes 196616 | tf_op jit(solution)/shard_map/ppermute | solution.py:25
  117.8 4.3 %collective-permute-start.7 = (f32[128,128]{1,0:T(8,128)S(1)}, f32[128,128]{1,0:T(8,128)S(1)}, u32[]{:S(2)}, u32[]{:S(2)}) collective-permute-start(f32[128,128]{1,0:T(8,128)S(1)} %collective-permute-done.6), channel_id=1, source_target_pairs={{0,1},{1,2},{2,3},{3,4},{4,5},{5,6},{6,7},{7,8},{8,9},{9,10},{10,1... | collective-permute-start | bytes 196616 | tf_op jit(solution)/shard_map/ppermute | solution.py:25
  117.9 4.9 %collective-permute-start.3 = (f32[128,128]{1,0:T(8,128)S(1)}, f32[128,128]{1,0:T(8,128)S(1)}, u32[]{:S(2)}, u32[]{:S(2)}) collective-permute-start(f32[128,128]{1,0:T(8,128)S(1)} %collective-permute-done.2), channel_id=1, source_target_pairs={{0,1},{1,2},{2,3},{3,4},{4,5},{5,6},{6,7},{7,8},{8,9},{9,10},{10,1... | collective-permute-start | bytes 196616 | tf_op jit(solution)/shard_map/ppermute | solution.py:25
  122.2 4.3 %collective-permute-start.8 = (f32[128,128]{1,0:T(8,128)S(1)}, f32[128,128]{1,0:T(8,128)S(1)}, u32[]{:S(2)}, u32[]{:S(2)}) collective-permute-start(f32[128,128]{1,0:T(8,128)S(1)} %collective-permute-done.7), channel_id=1, source_target_pairs={{0,1},{1,2},{2,3},{3,4},{4,5},{5,6},{6,7},{7,8},{8,9},{9,10},{10,1... | collective-permute-start | bytes 196616 | tf_op jit(solution)/shard_map/ppermute | solution.py:25
  122.9 5.7 %collective-permute-start.4 = (f32[128,128]{1,0:T(8,128)S(1)}, f32[128,128]{1,0:T(8,128)S(1)}, u32[]{:S(2)}, u32[]{:S(2)}) collective-permute-start(f32[128,128]{1,0:T(8,128)S(1)} %collective-permute-done.3), channel_id=1, source_target_pairs={{0,1},{1,2},{2,3},{3,4},{4,5},{5,6},{6,7},{7,8},{8,9},{9,10},{10,1... | collective-permute-start | bytes 196616 | tf_op jit(solution)/shard_map/ppermute | solution.py:25
  126.4 7.3 %collective-permute-start.9 = (f32[128,128]{1,0:T(8,128)S(1)}, f32[128,128]{1,0:T(8,128)S(1)}, u32[]{:S(2)}, u32[]{:S(2)}) collective-permute-start(f32[128,128]{1,0:T(8,128)S(1)} %collective-permute-done.8), channel_id=1, source_target_pairs={{0,1},{1,2},{2,3},{3,4},{4,5},{5,6},{6,7},{7,8},{8,9},{9,10},{10,1... | collective-permute-start | bytes 196616 | tf_op jit(solution)/shard_map/ppermute | solution.py:25
  129.5 0.8 copy-start.3
  134.6 1.0 copy-start.2
  136.0 10.9 %collective-permute-start.23 = (f32[128,128]{1,0:T(8,128)S(1)}, f32[128,128]{1,0:T(8,128)S(1)}, u32[]{:S(2)}, u32[]{:S(2)}) collective-permute-start(f32[128,128]{1,0:T(8,128)S(1)} %convolution_bitcast_fusion.11), channel_id=1, source_target_pairs={{0,15},{1,0},{2,1},{3,2},{4,3},{5,4},{6,5},{7,6},{8,7},{9,8},{10,9... | collective-permute-start | bytes 196616 | tf_op jit(solution)/shard_map/ppermute | solution.py:25
  141.0 8.0 %collective-permute-start.18 = (f32[128,128]{1,0:T(8,128)S(1)}, f32[128,128]{1,0:T(8,128)S(1)}, u32[]{:S(2)}, u32[]{:S(2)}) collective-permute-start(f32[128,128]{1,0:T(8,128)S(1)} %fusion.54), channel_id=1, source_target_pairs={{0,15},{1,0},{2,1},{3,2},{4,3},{5,4},{6,5},{7,6},{8,7},{9,8},{10,9... | collective-permute-start | bytes 196616 | tf_op jit(solution)/shard_map/ppermute | solution.py:25
  142.2 4.3 %collective-permute-start.10 = (f32[128,128]{1,0:T(8,128)S(1)}, f32[128,128]{1,0:T(8,128)S(1)}, u32[]{:S(2)}, u32[]{:S(2)}) collective-permute-start(f32[128,128]{1,0:T(8,128)S(1)} %collective-permute-done.4), channel_id=1, source_target_pairs={{0,15},{1,0},{2,1},{3,2},{4,3},{5,4},{6,5},{7,6},{8,7},{9,8},{10,9... | collective-permute-start | bytes 196616 | tf_op jit(solution)/shard_map/ppermute | solution.py:25
  142.2 6.4 %collective-permute-start.11 = (f32[128,128]{1,0:T(8,128)S(1)}, f32[128,128]{1,0:T(8,128)S(1)}, u32[]{:S(2)}, u32[]{:S(2)}) collective-permute-start(f32[128,128]{1,0:T(8,128)S(1)} %collective-permute-done.9), channel_id=1, source_target_pairs={{0,15},{1,0},{2,1},{3,2},{4,3},{5,4},{6,5},{7,6},{8,7},{9,8},{10,9... | collective-permute-start | bytes 196616 | tf_op jit(solution)/shard_map/ppermute | solution.py:25
  147.3 10.0 %collective-permute-start.24 = (f32[128,128]{1,0:T(8,128)S(1)}, f32[128,128]{1,0:T(8,128)S(1)}, u32[]{:S(2)}, u32[]{:S(2)}) collective-permute-start(f32[128,128]{1,0:T(8,128)S(1)} %fusion.56), channel_id=1, source_target_pairs={{0,15},{1,0},{2,1},{3,2},{4,3},{5,4},{6,5},{7,6},{8,7},{9,8},{10,9... | collective-permute-start | bytes 196616 | tf_op jit(solution)/shard_map/ppermute | solution.py:25
  149.4 10.5 %collective-permute-start.19 = (f32[128,128]{1,0:T(8,128)S(1)}, f32[128,128]{1,0:T(8,128)S(1)}, u32[]{:S(2)}, u32[]{:S(2)}) collective-permute-start(f32[128,128]{1,0:T(8,128)S(1)} %fusion.55), channel_id=1, source_target_pairs={{0,15},{1,0},{2,1},{3,2},{4,3},{5,4},{6,5},{7,6},{8,7},{9,8},{10,9... | collective-permute-start | bytes 196616 | tf_op jit(solution)/shard_map/ppermute | solution.py:25
  151.7 4.8 %collective-permute-start.12 = (f32[128,128]{1,0:T(8,128)S(1)}, f32[128,128]{1,0:T(8,128)S(1)}, u32[]{:S(2)}, u32[]{:S(2)}) collective-permute-start(f32[128,128]{1,0:T(8,128)S(1)} %collective-permute-done.10), channel_id=1, source_target_pairs={{0,15},{1,0},{2,1},{3,2},{4,3},{5,4},{6,5},{7,6},{8,7},{9,8},{10,9... | collective-permute-start | bytes 196616 | tf_op jit(solution)/shard_map/ppermute | solution.py:25
  151.8 7.4 %collective-permute-start.13 = (f32[128,128]{1,0:T(8,128)S(1)}, f32[128,128]{1,0:T(8,128)S(1)}, u32[]{:S(2)}, u32[]{:S(2)}) collective-permute-start(f32[128,128]{1,0:T(8,128)S(1)} %collective-permute-done.11), channel_id=1, source_target_pairs={{0,15},{1,0},{2,1},{3,2},{4,3},{5,4},{6,5},{7,6},{8,7},{9,8},{10,9... | collective-permute-start | bytes 196616 | tf_op jit(solution)/shard_map/ppermute | solution.py:25
  157.3 10.2 %collective-permute-start.25 = (f32[128,128]{1,0:T(8,128)S(1)}, f32[128,128]{1,0:T(8,128)S(1)}, u32[]{:S(2)}, u32[]{:S(2)}) collective-permute-start(f32[128,128]{1,0:T(8,128)S(1)} %add.357), channel_id=1, source_target_pairs={{0,15},{1,0},{2,1},{3,2},{4,3},{5,4},{6,5},{7,6},{8,7},{9,8},{10,9... | collective-permute-start | bytes 196616 | tf_op jit(solution)/shard_map/ppermute | solution.py:25
  159.9 10.1 %collective-permute-start.20 = (f32[128,128]{1,0:T(8,128)S(1)}, f32[128,128]{1,0:T(8,128)S(1)}, u32[]{:S(2)}, u32[]{:S(2)}) collective-permute-start(f32[128,128]{1,0:T(8,128)S(1)} %add.351), channel_id=1, source_target_pairs={{0,15},{1,0},{2,1},{3,2},{4,3},{5,4},{6,5},{7,6},{8,7},{9,8},{10,9... | collective-permute-start | bytes 196616 | tf_op jit(solution)/shard_map/ppermute | solution.py:25
  161.9 4.9 %collective-permute-start.14 = (f32[128,128]{1,0:T(8,128)S(1)}, f32[128,128]{1,0:T(8,128)S(1)}, u32[]{:S(2)}, u32[]{:S(2)}) collective-permute-start(f32[128,128]{1,0:T(8,128)S(1)} %collective-permute-done.12), channel_id=1, source_target_pairs={{0,15},{1,0},{2,1},{3,2},{4,3},{5,4},{6,5},{7,6},{8,7},{9,8},{10,9... | collective-permute-start | bytes 196616 | tf_op jit(solution)/shard_map/ppermute | solution.py:25
  162.4 6.8 %collective-permute-start.15 = (f32[128,128]{1,0:T(8,128)S(1)}, f32[128,128]{1,0:T(8,128)S(1)}, u32[]{:S(2)}, u32[]{:S(2)}) collective-permute-start(f32[128,128]{1,0:T(8,128)S(1)} %collective-permute-done.13), channel_id=1, source_target_pairs={{0,15},{1,0},{2,1},{3,2},{4,3},{5,4},{6,5},{7,6},{8,7},{9,8},{10,9... | collective-permute-start | bytes 196616 | tf_op jit(solution)/shard_map/ppermute | solution.py:25
  167.6 67.7 %collective-permute-start.26 = (f32[128,128]{1,0:T(8,128)S(1)}, f32[128,128]{1,0:T(8,128)S(1)}, u32[]{:S(2)}, u32[]{:S(2)}) collective-permute-start(f32[128,128]{1,0:T(8,128)S(1)} %add.358), channel_id=1, source_target_pairs={{0,15},{1,0},{2,1},{3,2},{4,3},{5,4},{6,5},{7,6},{8,7},{9,8},{10,9... | collective-permute-start | bytes 196616 | tf_op jit(solution)/shard_map/ppermute | solution.py:25
  170.1 67.7 %collective-permute-start.21 = (f32[128,128]{1,0:T(8,128)S(1)}, f32[128,128]{1,0:T(8,128)S(1)}, u32[]{:S(2)}, u32[]{:S(2)}) collective-permute-start(f32[128,128]{1,0:T(8,128)S(1)} %add.352), channel_id=1, source_target_pairs={{0,15},{1,0},{2,1},{3,2},{4,3},{5,4},{6,5},{7,6},{8,7},{9,8},{10,9... | collective-permute-start | bytes 196616 | tf_op jit(solution)/shard_map/ppermute | solution.py:25
  172.9 4.3 %collective-permute-start.16 = (f32[128,128]{1,0:T(8,128)S(1)}, f32[128,128]{1,0:T(8,128)S(1)}, u32[]{:S(2)}, u32[]{:S(2)}) collective-permute-start(f32[128,128]{1,0:T(8,128)S(1)} %collective-permute-done.14), channel_id=1, source_target_pairs={{0,15},{1,0},{2,1},{3,2},{4,3},{5,4},{6,5},{7,6},{8,7},{9,8},{10,9... | collective-permute-start | bytes 196616 | tf_op jit(solution)/shard_map/ppermute | solution.py:25
  173.1 63.9 %collective-permute-start.17 = (f32[128,128]{1,0:T(8,128)S(1)}, f32[128,128]{1,0:T(8,128)S(1)}, u32[]{:S(2)}, u32[]{:S(2)}) collective-permute-start(f32[128,128]{1,0:T(8,128)S(1)} %collective-permute-done.15), channel_id=1, source_target_pairs={{0,15},{1,0},{2,1},{3,2},{4,3},{5,4},{6,5},{7,6},{8,7},{9,8},{10,9... | collective-permute-start | bytes 196616 | tf_op jit(solution)/shard_map/ppermute | solution.py:25
  235.4 4.8 %collective-permute-start.27 = (f32[128,64]{1,0:T(8,128)S(1)}, f32[128,64]{1,0:T(8,128)S(1)}, u32[]{:S(2)}, u32[]{:S(2)}) collective-permute-start(f32[128,64]{1,0:T(8,128)S(1)} %slice_select_fusion), channel_id=1, source_target_pairs={{0,16},{16,0},{1,17},{17,1},{2,18},{18,2},{3,19},{19,3},{4,20},{20... | collective-permute-start | bytes 98312 | tf_op jit(solution)/shard_map/ppermute | solution.py:14
  237.3 0.8 copy-start.4
  238.3 4.3 %collective-permute-start.22 = (f32[128,64]{1,0:T(8,128)S(1)}, f32[128,64]{1,0:T(8,128)S(1)}, u32[]{:S(2)}, u32[]{:S(2)}) collective-permute-start(f32[128,64]{1,0:T(8,128)S(1)} %slice_select_fusion.1), channel_id=1, source_target_pairs={{0,16},{16,0},{1,17},{17,1},{2,18},{18,2},{3,19},{19,3},{4,20},{20... | collective-permute-start | bytes 98312 | tf_op jit(solution)/shard_map/ppermute | solution.py:14
Sparse Core Ops, SparseCore 0:
  26.0 90.5 all-reduce.6
  142.3 92.9 all-reduce.4
where the time goes:
time: 251 us; the launch traced here: 250 us
  waiting for transfers between devices  169 us (67%)
  starting transfers between devices  31.6 us (13%)
  between operations  22.4 us (9%)
  matrix products  18.4 us (7%)
  local copies, waits for them, and re-layouts  5.47 us (2%)
  other arithmetic  3.54 us (1%)
    psum x1, waiting for transfers between devices, spread(): return lax.psum(jnp.where(mine, array, jnp.zeros_like(array)), axis)  88.4 us
    psum x1, waiting for transfers between devices, shards(): total_dk, total_dv = lax.psum((sink_dk, sink_dv), ('inner', 'outer'))  57.4 us
    ppermute x24, starting transfers between devices, shifted(): return lax.ppermute(value, axis, pairs)  27.2 us
    ppermute x24, waiting for transfers between devices, shifted(): return lax.ppermute(value, axis, pairs)  21.4 us
  transfers between devices with their start and end apart: 30, of which 12 were waited for; matrix products, arithmetic and copies ran while one was open for 9% of the time, Pallas kernels for 0%

commit v1 on v0

--- a/solution.py
+++ b/solution.py
@@ -1,3 +1,4 @@
+import functools
 import math
 import jax
 import jax.numpy as jnp
@@ -8,6 +9,15 @@
 SINK = 128
 very_low = -1e30
 precise = lax.Precision.HIGHEST
+
+
+def _build_series(load, dev_axis, mesh_dim):
+    for it in (dev_axis, mesh_dim):
+        load = lax.psum(load, axis_name=it)
+    return load
+
+
+choose_zones = functools.partial(_build_series, dev_axis="outer", mesh_dim="inner")
 
 
 def swapped(array, axis, distance):
@@ -160,7 +170,7 @@
         queries, out_grad, log_sum, row_delta, sink_keys, sink_values, sink_allowed, temper, None
     )
     grad_q = grad_q + sink_dq
-    total_dk, total_dv = lax.psum((sink_dk, sink_dv), ("inner", "outer"))
+    total_dk, total_dv = choose_zones((sink_dk, sink_dv))
     is_first = seq_index == 0
     grad_keys = grad_keys.at[:SINK].add(jnp.where(is_first, total_dk, 0.0))
     grad_values = grad_values.at[:SINK].add(jnp.where(is_first, total_dv, 0.0))

time: 251 us -> 229 us (0.912); the launches traced: 250 us -> 226 us
  waiting for transfers between devices: 169 us -> 144 us
    psum x1 -> x2, waiting for transfers between devices: 57.4 us -> 34.1 us  [_build_series(): load = lax.psum(load, axis_name=it)]
  transfers between devices with their start and end apart: 30 -> 31, of which waited for: 12 -> 13; matrix products, arithmetic and copies ran while one was open for 9% -> 10% of each run, Pallas kernels for 0% -> 0%
where the time goes in v1:
time: 229 us; the launch traced here: 226 us
  waiting for transfers between devices  144 us (63%)
  starting transfers between devices  31.9 us (14%)
  between operations  22.2 us (10%)
  matrix products  18.4 us (8%)
  local copies, waits for them, and re-layouts  5.47 us (2%)
  other arithmetic  3.62 us (2%)
    psum x1, waiting for transfers between devices, spread(): return lax.psum(jnp.where(mine, array, jnp.zeros_like(array)), axis)  88.4 us
    psum x2, waiting for transfers between devices, _build_series(): load = lax.psum(load, axis_name=it)  34.1 us
    ppermute x24, starting transfers between devices, shifted(): return lax.ppermute(value, axis, pairs)  27.4 us
    ppermute x24, waiting for transfers between devices, shifted(): return lax.ppermute(value, axis, pairs)  20 us
    dot_general x10, matrix products, scores(): jnp.einsum('qhd,kd->hqk', query_blk, key_blk, precision=precise)  4.88 us
    unnamed x20, local copies, waits for them, and re-layouts  4.87 us
  transfers between devices with their start and end apart: 31, of which 13 were waited for; matrix products, arithmetic and copies ran while one was open for 10% of the time, Pallas kernels for 0%

profile of v1, /device:TPU:8, one launch (start us, length us, event | category | flops | bytes accessed | tf_op | source)
XLA Modules:
  0.0 225.7 jit_solution(6699235813355351526)
XLA Ops:
  7.2 0.9 copy.10
  8.1 1.6 collective-permute-start
  9.8 0.6 collective-permute-start.5
  10.4 0.7 copy-done.6
  11.1 0.8 fusion.159
  20.9 0.7 broadcast_select_fusion.1
  21.7 1.6 collective-permute-start.1
  23.3 0.7 broadcast_select_fusion
  24.0 1.6 collective-permute-start.6
  26.3 1.6 collective-permute-start.2
  28.3 88.4 %all-reduce.7.cloned.1.call-done = (f32[128,128]{1,0:T(8,128)}, f32[128,128]{1,0:T(8,128)}) async-done(((f32[128,128]{1,0:T(8,128)}, f32[128,128]{1,0:T(8,128)}), (f32[128,128]{1,0:T(8,128)}, f32[128,128]{1,0:T(8,128)})) %all-reduce.7.cloned.1.call-update) | async-done | bytes 131088 | tf_op jit(solution)/shard_map/psum | solution.py:29
  116.7 1.2 select_reduce_fusion
  118.1 2.0 collective-permute-start.3
  120.5 1.8 collective-permute-done.7
  122.4 0.7 collective-permute-done.3
  123.0 1.3 collective-permute-start.4
  124.7 1.9 collective-permute-done.8
  126.6 0.7 collective-permute-start.9
  127.3 1.4 collective-permute-done.4
  130.5 0.5 fusion.20
  131.5 0.4 fusion.18
  131.9 0.4 fusion.17
  132.8 1.1 convolution_bitcast_fusion.6
  133.9 0.4 fusion.48
  134.7 1.0 fusion.49
  136.2 4.2 %collective-permute-start.23 = (f32[128,128]{1,0:T(8,128)S(1)}, f32[128,128]{1,0:T(8,128)S(1)}, u32[]{:S(2)}, u32[]{:S(2)}) collective-permute-start(f32[128,128]{1,0:T(8,128)S(1)} %convolution_bitcast_fusion.11), channel_id=1, source_target_pairs={{0,15},{1,0},{2,1},{3,2},{4,3},{5,4},{6,5},{7,6},{8,7},{9,8},{10,9... | collective-permute-start | bytes 196616 | tf_op jit(solution)/shard_map/ppermute | solution.py:35
  141.2 1.1 collective-permute-start.18
  143.0 3.8 %collective-permute-done.10 = f32[128,128]{1,0:T(8,128)S(1)} collective-permute-done((f32[128,128]{1,0:T(8,128)S(1)}, f32[128,128]{1,0:T(8,128)S(1)}, u32[]{:S(2)}, u32[]{:S(2)}) %collective-permute-start.10) | collective-permute-done | bytes 65568 | tf_op jit(solution)/shard_map/ppermute | solution.py:35
  147.5 1.2 collective-permute-start.24
  149.5 2.3 %collective-permute-start.19 = (f32[128,128]{1,0:T(8,128)S(1)}, f32[128,128]{1,0:T(8,128)S(1)}, u32[]{:S(2)}, u32[]{:S(2)}) collective-permute-start(f32[128,128]{1,0:T(8,128)S(1)} %fusion.55), channel_id=1, source_target_pairs={{0,15},{1,0},{2,1},{3,2},{4,3},{5,4},{6,5},{7,6},{8,7},{9,8},{10,9... | collective-permute-start | bytes 196616 | tf_op jit(solution)/shard_map/ppermute | solution.py:35
  152.4 4.3 %collective-permute-done.12 = f32[128,128]{1,0:T(8,128)S(1)} collective-permute-done((f32[128,128]{1,0:T(8,128)S(1)}, f32[128,128]{1,0:T(8,128)S(1)}, u32[]{:S(2)}, u32[]{:S(2)}) %collective-permute-start.12) | collective-permute-done | bytes 65568 | tf_op jit(solution)/shard_map/ppermute | solution.py:35
  157.6 1.3 collective-permute-start.25
  159.7 2.6 %collective-permute-start.20 = (f32[128,128]{1,0:T(8,128)S(1)}, f32[128,128]{1,0:T(8,128)S(1)}, u32[]{:S(2)}, u32[]{:S(2)}) collective-permute-start(f32[128,128]{1,0:T(8,128)S(1)} %add.355), channel_id=1, source_target_pairs={{0,15},{1,0},{2,1},{3,2},{4,3},{5,4},{6,5},{7,6},{8,7},{9,8},{10,9... | collective-permute-start | bytes 196616 | tf_op jit(solution)/shard_map/ppermute | solution.py:35
  162.2 14.7 %all-reduce.9.cloned.1.call-done = (f32[128,128]{1,0:T(8,128)}, f32[128,128]{1,0:T(8,128)}) async-done(((f32[128,128]{1,0:T(8,128)}, f32[128,128]{1,0:T(8,128)}), (f32[128,128]{1,0:T(8,128)}, f32[128,128]{1,0:T(8,128)})) %all-reduce.9.cloned.1.call-update) | async-done | bytes 131088 | tf_op jit(solution)/shard_map/psum | solution.py:16
  176.9 0.7 collective-permute-start.14
  177.6 0.5 collective-permute-start.15
  178.5 2.7 %collective-permute-done.14 = f32[128,128]{1,0:T(8,128)S(1)} collective-permute-done((f32[128,128]{1,0:T(8,128)S(1)}, f32[128,128]{1,0:T(8,128)S(1)}, u32[]{:S(2)}, u32[]{:S(2)}) %collective-permute-start.14) | collective-permute-done | bytes 65568 | tf_op jit(solution)/shard_map/ppermute | solution.py:35
  182.1 0.7 collective-permute-start.26
  183.6 2.7 %collective-permute-start.21 = (f32[128,128]{1,0:T(8,128)S(1)}, f32[128,128]{1,0:T(8,128)S(1)}, u32[]{:S(2)}, u32[]{:S(2)}) collective-permute-start(f32[128,128]{1,0:T(8,128)S(1)} %add.356), channel_id=1, source_target_pairs={{0,15},{1,0},{2,1},{3,2},{4,3},{5,4},{6,5},{7,6},{8,7},{9,8},{10,9... | collective-permute-start | bytes 196616 | tf_op jit(solution)/shard_map/ppermute | solution.py:35
  186.2 1.0 collective-permute-start.16
  187.7 3.1 %collective-permute-done.16 = f32[128,128]{1,0:T(8,128)S(1)} collective-permute-done((f32[128,128]{1,0:T(8,128)S(1)}, f32[128,128]{1,0:T(8,128)S(1)}, u32[]{:S(2)}, u32[]{:S(2)}) %collective-permute-start.16) | collective-permute-done | bytes 65568 | tf_op jit(solution)/shard_map/ppermute | solution.py:35
  191.7 19.4 %all-reduce.11.cloned.1.call-done = (f32[128,128]{1,0:T(8,128)}, f32[128,128]{1,0:T(8,128)}) async-done(((f32[128,128]{1,0:T(8,128)}, f32[128,128]{1,0:T(8,128)}), (f32[128,128]{1,0:T(8,128)}, f32[128,128]{1,0:T(8,128)})) %all-reduce.11.cloned.1.call-update) | async-done | bytes 131088 | tf_op jit(solution)/shard_map/psum | solution.py:16
  211.2 1.5 collective-permute-start.27
  214.1 0.6 collective-permute-start.22
  215.1 0.8 copy.78
  216.0 0.7 copy.80
  216.7 1.6 collective-permute-done.22
  218.5 0.7 copy.79
  (115 shorter events, 17.2 us)
Async XLA Ops:
  7.2 18.4 %copy-start = (f32[128,4,128]{2,1,0:T(4,128)S(1)}, f32[128,4,128]{2,1,0:T(4,128)}, u32[]{:S(2)}) copy-start(f32[128,4,128]{2,1,0:T(4,128)} %param.15) | copy-start | bytes 786436
  7.2 2.5 %copy-start.5 = (f32[128,64]{0,1:T(8,128)S(1)}, f32[128,64]{0,1:T(8,128)}, u32[]{:S(2)}) copy-start(f32[128,64]{0,1:T(8,128)} %param.17) | copy-start | bytes 98308
  7.2 109.5 %all-reduce.7.cloned.1.call-start = ((), (), s32[]{:S(2)}) async-start(), calls=%async_computation | async-start | bytes 262144 | tf_op jit(solution)/shard_map/psum | solution.py:29
  8.1 12.8 %collective-permute-start = (f32[128,64]{1,0:T(8,128)S(1)}, f32[128,64]{1,0:T(8,128)S(1)}, u32[]{:S(2)}, u32[]{:S(2)}) collective-permute-start(f32[128,64]{1,0:T(8,128)S(1)} %copy.10), channel_id=1, source_target_pairs={{0,16},{16,0},{1,17},{17,1},{2,18},{18,2},{3,19},{19,3},{4,20},{20... | collective-permute-start | bytes 98312 | tf_op jit(solution)/shard_map/ppermute | solution.py:24
  9.8 13.5 %collective-permute-start.5 = (f32[128,64]{1,0:T(8,128)S(1)}, f32[128,64]{1,0:T(8,128)S(1)}, u32[]{:S(2)}, u32[]{:S(2)}) collective-permute-start(f32[128,64]{1,0:T(8,128)S(1)} %copy.24), channel_id=1, source_target_pairs={{0,16},{16,0},{1,17},{17,1},{2,18},{18,2},{3,19},{19,3},{4,20},{20... | collective-permute-start | bytes 98312 | tf_op jit(solution)/shard_map/ppermute | solution.py:24
  10.4 0.7 copy-start.6
  10.4 10.4 %copy-start.1 = (f32[128,4,128]{2,1,0:T(4,128)S(1)}, f32[128,4,128]{2,1,0:T(4,128)}, u32[]{:S(2)}) copy-start(f32[128,4,128]{2,1,0:T(4,128)} %param.18) | copy-start | bytes 786436
  21.7 4.6 %collective-permute-start.1 = (f32[128,128]{1,0:T(8,128)S(1)}, f32[128,128]{1,0:T(8,128)S(1)}, u32[]{:S(2)}, u32[]{:S(2)}) collective-permute-start(f32[128,128]{1,0:T(8,128)S(1)} %get-tuple-element.82), channel_id=1, source_target_pairs={{0,1},{1,2},{2,3},{3,4},{4,5},{5,6},{6,7},{7,8},{8,9},{9,10},{10,1... | collective-permute-start | bytes 196616 | tf_op jit(solution)/shard_map/ppermute | solution.py:35
  24.0 94.0 %collective-permute-start.6 = (f32[128,128]{1,0:T(8,128)S(1)}, f32[128,128]{1,0:T(8,128)S(1)}, u32[]{:S(2)}, u32[]{:S(2)}) collective-permute-start(f32[128,128]{1,0:T(8,128)S(1)} %get-tuple-element.80), channel_id=1, source_target_pairs={{0,1},{1,2},{2,3},{3,4},{4,5},{5,6},{6,7},{7,8},{8,9},{9,10},{10,1... | collective-permute-start | bytes 196616 | tf_op jit(solution)/shard_map/ppermute | solution.py:35
  26.0 150.9 %all-reduce.9.cloned.1.call-start = ((), (), s32[]{:S(2)}) async-start(), calls=%async_computation.1 | async-start | bytes 262144 | tf_op jit(solution)/shard_map/psum | solution.py:16
  26.3 91.8 %collective-permute-start.2 = (f32[128,128]{1,0:T(8,128)S(1)}, f32[128,128]{1,0:T(8,128)S(1)}, u32[]{:S(2)}, u32[]{:S(2)}) collective-permute-start(f32[128,128]{1,0:T(8,128)S(1)} %collective-permute-done.1), channel_id=1, source_target_pairs={{0,1},{1,2},{2,3},{3,4},{4,5},{5,6},{6,7},{7,8},{8,9},{9,10},{10,1... | collective-permute-start | bytes 196616 | tf_op jit(solution)/shard_map/ppermute | solution.py:35
  118.0 4.3 %collective-permute-start.7 = (f32[128,128]{1,0:T(8,128)S(1)}, f32[128,128]{1,0:T(8,128)S(1)}, u32[]{:S(2)}, u32[]{:S(2)}) collective-permute-start(f32[128,128]{1,0:T(8,128)S(1)} %collective-permute-done.6), channel_id=1, source_target_pairs={{0,1},{1,2},{2,3},{3,4},{4,5},{5,6},{6,7},{7,8},{8,9},{9,10},{10,1... | collective-permute-start | bytes 196616 | tf_op jit(solution)/shard_map/ppermute | solution.py:35
  118.1 4.9 %collective-permute-start.3 = (f32[128,128]{1,0:T(8,128)S(1)}, f32[128,128]{1,0:T(8,128)S(1)}, u32[]{:S(2)}, u32[]{:S(2)}) collective-permute-start(f32[128,128]{1,0:T(8,128)S(1)} %collective-permute-done.2), channel_id=1, source_target_pairs={{0,1},{1,2},{2,3},{3,4},{4,5},{5,6},{6,7},{7,8},{8,9},{9,10},{10,1... | collective-permute-start | bytes 196616 | tf_op jit(solution)/shard_map/ppermute | solution.py:35
  122.3 4.3 %collective-permute-start.8 = (f32[128,128]{1,0:T(8,128)S(1)}, f32[128,128]{1,0:T(8,128)S(1)}, u32[]{:S(2)}, u32[]{:S(2)}) collective-permute-start(f32[128,128]{1,0:T(8,128)S(1)} %collective-permute-done.7), channel_id=1, source_target_pairs={{0,1},{1,2},{2,3},{3,4},{4,5},{5,6},{6,7},{7,8},{8,9},{9,10},{10,1... | collective-permute-start | bytes 196616 | tf_op jit(solution)/shard_map/ppermute | solution.py:35
  123.0 5.7 %collective-permute-start.4 = (f32[128,128]{1,0:T(8,128)S(1)}, f32[128,128]{1,0:T(8,128)S(1)}, u32[]{:S(2)}, u32[]{:S(2)}) collective-permute-start(f32[128,128]{1,0:T(8,128)S(1)} %collective-permute-done.3), channel_id=1, source_target_pairs={{0,1},{1,2},{2,3},{3,4},{4,5},{5,6},{6,7},{7,8},{8,9},{9,10},{10,1... | collective-permute-start | bytes 196616 | tf_op jit(solution)/shard_map/ppermute | solution.py:35
  126.6 7.3 %collective-permute-start.9 = (f32[128,128]{1,0:T(8,128)S(1)}, f32[128,128]{1,0:T(8,128)S(1)}, u32[]{:S(2)}, u32[]{:S(2)}) collective-permute-start(f32[128,128]{1,0:T(8,128)S(1)} %collective-permute-done.8), channel_id=1, source_target_pairs={{0,1},{1,2},{2,3},{3,4},{4,5},{5,6},{6,7},{7,8},{8,9},{9,10},{10,1... | collective-permute-start | bytes 196616 | tf_op jit(solution)/shard_map/ppermute | solution.py:35
  129.7 0.8 copy-start.3
  134.7 1.0 copy-start.2
  136.2 10.9 %collective-permute-start.23 = (f32[128,128]{1,0:T(8,128)S(1)}, f32[128,128]{1,0:T(8,128)S(1)}, u32[]{:S(2)}, u32[]{:S(2)}) collective-permute-start(f32[128,128]{1,0:T(8,128)S(1)} %convolution_bitcast_fusion.11), channel_id=1, source_target_pairs={{0,15},{1,0},{2,1},{3,2},{4,3},{5,4},{6,5},{7,6},{8,7},{9,8},{10,9... | collective-permute-start | bytes 196616 | tf_op jit(solution)/shard_map/ppermute | solution.py:35
  141.2 8.0 %collective-permute-start.18 = (f32[128,128]{1,0:T(8,128)S(1)}, f32[128,128]{1,0:T(8,128)S(1)}, u32[]{:S(2)}, u32[]{:S(2)}) collective-permute-start(f32[128,128]{1,0:T(8,128)S(1)} %fusion.54), channel_id=1, source_target_pairs={{0,15},{1,0},{2,1},{3,2},{4,3},{5,4},{6,5},{7,6},{8,7},{9,8},{10,9... | collective-permute-start | bytes 196616 | tf_op jit(solution)/shard_map/ppermute | solution.py:35
  142.3 68.7 %all-reduce.11.cloned.1.call-start = ((), (), s32[]{:S(2)}) async-start(), calls=%async_computation.2 | async-start | bytes 262144 | tf_op jit(solution)/shard_map/psum | solution.py:16
  142.4 4.3 %collective-permute-start.10 = (f32[128,128]{1,0:T(8,128)S(1)}, f32[128,128]{1,0:T(8,128)S(1)}, u32[]{:S(2)}, u32[]{:S(2)}) collective-permute-start(f32[128,128]{1,0:T(8,128)S(1)} %collective-permute-done.4), channel_id=1, source_target_pairs={{0,15},{1,0},{2,1},{3,2},{4,3},{5,4},{6,5},{7,6},{8,7},{9,8},{10,9... | collective-permute-start | bytes 196616 | tf_op jit(solution)/shard_map/ppermute | solution.py:35
  142.5 6.3 %collective-permute-start.11 = (f32[128,128]{1,0:T(8,128)S(1)}, f32[128,128]{1,0:T(8,128)S(1)}, u32[]{:S(2)}, u32[]{:S(2)}) collective-permute-start(f32[128,128]{1,0:T(8,128)S(1)} %collective-permute-done.9), channel_id=1, source_target_pairs={{0,15},{1,0},{2,1},{3,2},{4,3},{5,4},{6,5},{7,6},{8,7},{9,8},{10,9... | collective-permute-start | bytes 196616 | tf_op jit(solution)/shard_map/ppermute | solution.py:35
  147.5 10.1 %collective-permute-start.24 = (f32[128,128]{1,0:T(8,128)S(1)}, f32[128,128]{1,0:T(8,128)S(1)}, u32[]{:S(2)}, u32[]{:S(2)}) collective-permute-start(f32[128,128]{1,0:T(8,128)S(1)} %fusion.56), channel_id=1, source_target_pairs={{0,15},{1,0},{2,1},{3,2},{4,3},{5,4},{6,5},{7,6},{8,7},{9,8},{10,9... | collective-permute-start | bytes 196616 | tf_op jit(solution)/shard_map/ppermute | solution.py:35
  149.5 10.1 %collective-permute-start.19 = (f32[128,128]{1,0:T(8,128)S(1)}, f32[128,128]{1,0:T(8,128)S(1)}, u32[]{:S(2)}, u32[]{:S(2)}) collective-permute-start(f32[128,128]{1,0:T(8,128)S(1)} %fusion.55), channel_id=1, source_target_pairs={{0,15},{1,0},{2,1},{3,2},{4,3},{5,4},{6,5},{7,6},{8,7},{9,8},{10,9... | collective-permute-start | bytes 196616 | tf_op jit(solution)/shard_map/ppermute | solution.py:35
  151.9 4.9 %collective-permute-start.12 = (f32[128,128]{1,0:T(8,128)S(1)}, f32[128,128]{1,0:T(8,128)S(1)}, u32[]{:S(2)}, u32[]{:S(2)}) collective-permute-start(f32[128,128]{1,0:T(8,128)S(1)} %collective-permute-done.10), channel_id=1, source_target_pairs={{0,15},{1,0},{2,1},{3,2},{4,3},{5,4},{6,5},{7,6},{8,7},{9,8},{10,9... | collective-permute-start | bytes 196616 | tf_op jit(solution)/shard_map/ppermute | solution.py:35
  151.9 7.0 %collective-permute-start.13 = (f32[128,128]{1,0:T(8,128)S(1)}, f32[128,128]{1,0:T(8,128)S(1)}, u32[]{:S(2)}, u32[]{:S(2)}) collective-permute-start(f32[128,128]{1,0:T(8,128)S(1)} %collective-permute-done.11), channel_id=1, source_target_pairs={{0,15},{1,0},{2,1},{3,2},{4,3},{5,4},{6,5},{7,6},{8,7},{9,8},{10,9... | collective-permute-start | bytes 196616 | tf_op jit(solution)/shard_map/ppermute | solution.py:35
  157.6 24.4 %collective-permute-start.25 = (f32[128,128]{1,0:T(8,128)S(1)}, f32[128,128]{1,0:T(8,128)S(1)}, u32[]{:S(2)}, u32[]{:S(2)}) collective-permute-start(f32[128,128]{1,0:T(8,128)S(1)} %add.361), channel_id=1, source_target_pairs={{0,15},{1,0},{2,1},{3,2},{4,3},{5,4},{6,5},{7,6},{8,7},{9,8},{10,9... | collective-permute-start | bytes 196616 | tf_op jit(solution)/shard_map/ppermute | solution.py:35
  159.7 23.8 %collective-permute-start.20 = (f32[128,128]{1,0:T(8,128)S(1)}, f32[128,128]{1,0:T(8,128)S(1)}, u32[]{:S(2)}, u32[]{:S(2)}) collective-permute-start(f32[128,128]{1,0:T(8,128)S(1)} %add.355), channel_id=1, source_target_pairs={{0,15},{1,0},{2,1},{3,2},{4,3},{5,4},{6,5},{7,6},{8,7},{9,8},{10,9... | collective-permute-start | bytes 196616 | tf_op jit(solution)/shard_map/ppermute | solution.py:35
  176.9 4.3 %collective-permute-start.14 = (f32[128,128]{1,0:T(8,128)S(1)}, f32[128,128]{1,0:T(8,128)S(1)}, u32[]{:S(2)}, u32[]{:S(2)}) collective-permute-start(f32[128,128]{1,0:T(8,128)S(1)} %collective-permute-done.12), channel_id=1, source_target_pairs={{0,15},{1,0},{2,1},{3,2},{4,3},{5,4},{6,5},{7,6},{8,7},{9,8},{10,9... | collective-permute-start | bytes 196616 | tf_op jit(solution)/shard_map/ppermute | solution.py:35
  177.6 5.2 %collective-permute-start.15 = (f32[128,128]{1,0:T(8,128)S(1)}, f32[128,128]{1,0:T(8,128)S(1)}, u32[]{:S(2)}, u32[]{:S(2)}) collective-permute-start(f32[128,128]{1,0:T(8,128)S(1)} %collective-permute-done.13), channel_id=1, source_target_pairs={{0,15},{1,0},{2,1},{3,2},{4,3},{5,4},{6,5},{7,6},{8,7},{9,8},{10,9... | collective-permute-start | bytes 196616 | tf_op jit(solution)/shard_map/ppermute | solution.py:35
  182.1 29.0 %collective-permute-start.26 = (f32[128,128]{1,0:T(8,128)S(1)}, f32[128,128]{1,0:T(8,128)S(1)}, u32[]{:S(2)}, u32[]{:S(2)}) collective-permute-start(f32[128,128]{1,0:T(8,128)S(1)} %add.362), channel_id=1, source_target_pairs={{0,15},{1,0},{2,1},{3,2},{4,3},{5,4},{6,5},{7,6},{8,7},{9,8},{10,9... | collective-permute-start | bytes 196616 | tf_op jit(solution)/shard_map/ppermute | solution.py:35
  183.6 30.0 %collective-permute-start.21 = (f32[128,128]{1,0:T(8,128)S(1)}, f32[128,128]{1,0:T(8,128)S(1)}, u32[]{:S(2)}, u32[]{:S(2)}) collective-permute-start(f32[128,128]{1,0:T(8,128)S(1)} %add.356), channel_id=1, source_target_pairs={{0,15},{1,0},{2,1},{3,2},{4,3},{5,4},{6,5},{7,6},{8,7},{9,8},{10,9... | collective-permute-start | bytes 196616 | tf_op jit(solution)/shard_map/ppermute | solution.py:35
  186.2 4.6 %collective-permute-start.16 = (f32[128,128]{1,0:T(8,128)S(1)}, f32[128,128]{1,0:T(8,128)S(1)}, u32[]{:S(2)}, u32[]{:S(2)}) collective-permute-start(f32[128,128]{1,0:T(8,128)S(1)} %collective-permute-done.14), channel_id=1, source_target_pairs={{0,15},{1,0},{2,1},{3,2},{4,3},{5,4},{6,5},{7,6},{8,7},{9,8},{10,9... | collective-permute-start | bytes 196616 | tf_op jit(solution)/shard_map/ppermute | solution.py:35
  187.2 25.5 %collective-permute-start.17 = (f32[128,128]{1,0:T(8,128)S(1)}, f32[128,128]{1,0:T(8,128)S(1)}, u32[]{:S(2)}, u32[]{:S(2)}) collective-permute-start(f32[128,128]{1,0:T(8,128)S(1)} %collective-permute-done.15), channel_id=1, source_target_pairs={{0,15},{1,0},{2,1},{3,2},{4,3},{5,4},{6,5},{7,6},{8,7},{9,8},{10,9... | collective-permute-start | bytes 196616 | tf_op jit(solution)/shard_map/ppermute | solution.py:35
  211.2 4.8 %collective-permute-start.27 = (f32[128,64]{1,0:T(8,128)S(1)}, f32[128,64]{1,0:T(8,128)S(1)}, u32[]{:S(2)}, u32[]{:S(2)}) collective-permute-start(f32[128,64]{1,0:T(8,128)S(1)} %slice_select_fusion), channel_id=1, source_target_pairs={{0,16},{16,0},{1,17},{17,1},{2,18},{18,2},{3,19},{19,3},{4,20},{20... | collective-permute-start | bytes 98312 | tf_op jit(solution)/shard_map/ppermute | solution.py:24
  213.1 0.8 copy-start.4
  214.1 4.3 %collective-permute-start.22 = (f32[128,64]{1,0:T(8,128)S(1)}, f32[128,64]{1,0:T(8,128)S(1)}, u32[]{:S(2)}, u32[]{:S(2)}) collective-permute-start(f32[128,64]{1,0:T(8,128)S(1)} %slice_select_fusion.1), channel_id=1, source_target_pairs={{0,16},{16,0},{1,17},{17,1},{2,18},{18,2},{3,19},{19,3},{4,20},{20... | collective-permute-start | bytes 98312 | tf_op jit(solution)/shard_map/ppermute | solution.py:24
Sparse Core Ops, SparseCore 0:
  26.1 90.5 all-reduce.6
  142.4 34.4 all-reduce.8
  179.3 31.7 all-reduce.10
